TPU v7x, 32 devices: a whole 2x2x4 slice. The times are simulated.
32 devices in a mesh: tm: 4 (over z), batch: 4 (over x, core), width: 2 (over y).
Axes of the slice: x: 2, y: 2, z: 4, core: 2. Of those that a mesh axis runs over, the one named last changes fastest.
Arguments:
- moves: int32 [8, 1024], P('batch', 'tm'), may hold values from 0 to 361
- lengths: int32 [8], P('batch'), may hold values from 1 to 1024
- outcomes: int32 [8], P('batch'), may hold values from -1 to 1
- embedded: bfloat16 [8, 1024, 2048], P('batch', 'tm', 'width'), may hold values from -6 to 6
- w_branches: bfloat16 [4, 2048, 2048], P(None, ('tm', 'batch'), 'width'), may hold values from -0.125 to 0.125
- conv_w: float32 [4, 2048], P(None, 'width'), may hold values from -3 to 3
- gate_bias: float32 [2, 2048], P(None, 'width'), may hold values from -4 to 4
- rates: float32 [2048], P('width'), may hold values from 0.001 to 0.105
- w_down: bfloat16 [2048, 2048], P(('tm', 'batch'), 'width'), may hold values from -0.125 to 0.125
- w_policy: bfloat16 [2048, 362], P('width'), may hold values from -12 to 12
- w_value: bfloat16 [2048], P('width'), may hold values from -0.125 to 0.125
Outputs:
- position_loss: float32 [8, 1024], P('batch', 'tm')
- value: float32 [8, 1024], P('batch', 'tm')
All inputs are finite; a program needn't handle non-finite values.
Results may differ from a plain program's by a relative error of at most 0.0033.
Values may be sent and summed in bfloat16 or wider, within the bound.
A program may use at most 128 MiB of HBM per device.

v0:
```python
import jax
import jax.numpy as jnp
from jax import lax
from jax.sharding import PartitionSpec as P

D = 2048
KERNEL = 4


def from_behind(value, axis, steps):
    count = lax.axis_size(axis)
    initial, last = (max(0, -steps), min(count, count - steps))
    return lax.ppermute(value, axis, [(source, source + steps) for source in range(initial, last)])


def link(early, late):
    return (early[0] + late[0], jnp.exp(late[0]) * early[1] + late[1])


def shards(
    moves,
    lengths,
    outcomes,
    embedded,
    w_branches,
    conv_w,
    gate_bias,
    rates,
    w_down,
    w_policy,
    w_value,
):
    games, block_len, half = embedded.shape
    count = games * block_len
    chans = w_branches.shape[2]
    features = lax.all_gather(embedded, "width", axis=2, tiled=True).reshape(count, -1)
    proj = jnp.einsum(
        "td,kdn->ktn",
        features,
        lax.all_gather(w_branches, ("tm", "batch"), axis=1, tiled=True),
        preferred_element_type=jnp.float32,
    )
    proj = proj.reshape(4, games, block_len, chans)
    gated = jax.nn.gelu(proj[0])
    source = proj[1]
    prior = from_behind(source[:, block_len - (KERNEL - 1) :, :], "tm", 1)
    extended = jnp.concatenate([prior, source], 1)
    conv = jnp.zeros((games, block_len, chans), jnp.float32)
    for k in range(KERNEL):
        conv = conv + conv_w[k] * extended[:, KERNEL - 1 - k : KERNEL - 1 - k + block_len]
    recur = jax.nn.sigmoid(proj[2] + gate_bias[0])
    inflow = jax.nn.sigmoid(proj[3] + gate_bias[1])
    log_a = -8.0 * recur * rates
    decay = jnp.exp(log_a)
    drive = jnp.sqrt(1.0 - decay * decay) * inflow * conv
    summed, local = lax.associative_scan(link, (log_a, drive), axis=1)
    block_decay = jnp.exp(summed[:, -1])
    block_end = local[:, -1]

    def relay(step, state):
        outgoing, _ = state
        arrived = from_behind(outgoing, "tm", 1)
        return (block_decay * arrived + block_end, arrived)

    _, incoming = lax.fori_loop(
        0, lax.axis_size("tm") - 1, relay, (block_end, jnp.zeros_like(block_end))
    )
    hidden = local + jnp.exp(summed) * incoming[:, None, :]
    mixed = (hidden * gated).astype(jnp.bfloat16).reshape(count, chans)
    partial_down = lax.dot_general(
        mixed,
        lax.all_gather(w_down, ("tm", "batch"), axis=0, tiled=True),
        (((1,), (1,)), ((), ())),
        preferred_element_type=jnp.float32,
    )
    down = lax.psum_scatter(partial_down, "width", scatter_dimension=1, tiled=True)
    resid = (embedded.reshape(count, half).astype(jnp.float32) + down).astype(jnp.bfloat16)
    wide = resid.astype(jnp.float32)
    local_sq = jnp.sum(wide * wide, -1)
    local_logits = jnp.dot(resid, w_policy, preferred_element_type=jnp.float32)
    local_value = jnp.dot(resid, w_value, preferred_element_type=jnp.float32)
    raw_logits, raw_value, sumsq = lax.psum((local_logits, local_value, local_sq), "width")
    norm = lax.rsqrt(sumsq / D + 1e-06)
    logits = raw_logits * norm[:, None]
    value = jnp.tanh(raw_value * norm)
    top = jnp.max(logits, -1, keepdims=True)
    lse = top[:, 0] + jnp.log(jnp.sum(jnp.exp(logits - top), -1))
    column = lax.broadcasted_iota(jnp.int32, logits.shape, 1)
    picked = jnp.sum(jnp.where(column == moves.reshape(count, 1), logits, 0.0), -1)
    target = jnp.broadcast_to(outcomes.astype(jnp.float32)[:, None], (games, block_len)).reshape(
        count
    )
    position = lax.axis_index("tm") * block_len + lax.broadcasted_iota(
        jnp.int32, (games, block_len), 1
    )
    where_live = (position < lengths[:, None]).reshape(count)
    loss = jnp.where(where_live, lse - picked + (value - target) ** 2, 0.0)
    return (loss.reshape(games, block_len), value.reshape(games, block_len))


def solution(mesh):
    in_specs = (
        P("batch", "tm"),
        P("batch"),
        P("batch"),
        P("batch", "tm", "width"),
        P(None, ("tm", "batch"), "width"),
        P(None, "width"),
        P(None, "width"),
        P("width"),
        P(("tm", "batch"), "width"),
        P("width", None),
        P("width"),
    )
    out_specs = (P("batch", "tm"), P("batch", "tm"))
    return jax.shard_map(shards, mesh=mesh, in_specs=in_specs, out_specs=out_specs, check_vma=False)
```

profile of v0, /device:TPU:0, one launch (start us, length us, event | category | flops | bytes accessed | tf_op | source)
XLA Modules:
  0.0 492.6 jit_solution(15699372225943647497)
XLA Ops:
  9.5 35.9 %all-gather.6.cloned.1.call-done = bf16[2,256,2048]{2,1,0:T(8,128)(2,1)} async-done(((bf16[2,256,1024]{2,1,0:T(8,128)(2,1)}), bf16[2,256,2048]{2,1,0:T(8,128)(2,1)}) %all-gather.6.cloned.1.call-update) | async-done | bytes 2097168 | tf_op jit(solution)/shard_map/all_gather | solution.py:36
  45.4 128.7 %all-gather.4.cloned.1.call-done = bf16[4,2048,1024]{2,1,0:T(8,128)(2,1)} async-done(((bf16[4,128,1024]{2,1,0:T(8,128)(2,1)}), bf16[4,2048,1024]{2,1,0:T(8,128)(2,1)}) %all-gather.4.cloned.1.call-update) | async-done | bytes 16777232 | tf_op jit(solution)/shard_map/all_gather | solution.py:40
  174.1 12.5 %convolution_bitcast_fusion = f32[4,512,1024]{2,1,0:T(8,128)S(1)} fusion(bf16[512,2048,1]{1,0,2:T(8,128)(2,1)} %bitcast.75, bf16[4,2048,1024]{2,1,0:T(8,128)(2,1)} %all-gather.4.cloned.1.call-done), kind=kOutput, calls=%fused_computation.1 | convolution fusion | flops 8589934592 | bytes 27262976 | tf_op jit(solution)/shard_map/td,kdn->ktn/dot_general | solution.py:37
  186.6 2.9 fusion.30
  190.9 1.8 collective-permute-start.1
  192.7 1.4 collective-permute-done.1
  194.2 7.6 %fusion.4 = (f32[2,256,1024]{2,1,0:T(8,128)S(1)}, f32[2,256,1024]{2,1,0:T(8,128)}) fusion(f32[2,3,1024]{2,1,0:T(4,128)S(1)} %collective-permute-done.1, f32[2,256,1024]{2,1,0:T(8,128)} %bitcast.47, f32[2,256,1024]{2,1,0:T(8,128)} %bitcast.50, f32[1024]{0:T(1024)S(1)} %bitcast.69, f32[1024]{0:T(1024)S(1)} %bitcast.70, f32[1024]{0:T(1024)S(1)} %bitcast.68, ...), kind=kLoop, calls=%fused_computation.9 | loop fusion | flops 12058624 | bytes 10539008 | tf_op jit(solution)/shard_map/mul | solution.py:55
  201.7 2.9 slice.298
  204.6 2.9 slice.299
  207.5 5.4 %slice.297 = f32[2,128,1024]{2,1,0:T(8,128)} slice(f32[2,256,1024]{2,1,0:T(8,128)} %get-tuple-element.48), slice={[0:2:1], [1:256:2], [0:1024:1]} | slice | bytes 2097152 | tf_op jit(solution)/shard_map/slice | solution.py:56
  212.9 5.5 %slice.301 = f32[2,128,1024]{2,1,0:T(8,128)} slice(f32[2,256,1024]{2,1,0:T(8,128)} %get-tuple-element.48), slice={[0:2:1], [0:255:2], [0:1024:1]} | slice | bytes 2097152 | tf_op jit(solution)/shard_map/slice | solution.py:56
  218.4 4.2 multiply_add_fusion.1
  222.5 3.3 slice.304
  225.8 3.3 slice.305
  229.1 3.3 slice.303
  232.3 3.2 slice.307
  235.6 2.5 multiply_add_fusion.2
  239.7 1.7 slice.309
  241.4 1.7 slice.313
  243.1 2.1 multiply_add_fusion.3
  245.1 1.6 slice.316
  246.8 1.6 slice.317
  248.4 1.6 slice.315
  250.0 1.6 slice.319
  251.6 1.8 multiply_add_fusion.4
  254.7 1.5 slice.321
  256.2 1.5 slice.325
  257.7 1.6 multiply_add_fusion.5
  259.4 1.5 slice.329
  260.8 1.5 slice.328
  262.3 1.5 slice.327
  263.7 1.5 slice.331
  270.0 1.5 slice.326
  271.5 1.5 slice.343
  275.8 1.5 slice.320
  278.0 1.4 slice.410
  281.1 1.6 slice.347
  285.6 1.7 slice.308
  290.1 3.3 slice.302
  293.4 3.3 slice.351
  299.6 5.6 %slice.296 = f32[2,127,1024]{2,1,0:T(8,128)} slice(f32[2,256,1024]{2,1,0:T(8,128)} %get-tuple-element.48), slice={[0:2:1], [2:256:2], [0:1024:1]} | slice | bytes 2080768 | tf_op jit(solution)/shard_map/slice | solution.py:56
  305.2 3.0 slice.353
  308.2 1.4 slice.406
  318.5 5.5 %pad.129 = f32[2,256,1024]{2,1,0:T(8,128)} pad(f32[2,128,1024]{2,1,0:T(8,128)} %add.338, f32[]{:T(128)} %constant.6.clone.1), padding=0_0_0x1_0_1x0_0_0 | pad | bytes 3145732 | tf_op jit(solution)/shard_map/pad | solution.py:56
  323.9 1.9 pad_maximum_fusion.3
  325.8 3.0 pad.110
  328.8 2.0 pad.111
  330.9 2.9 add.322
  333.7 2.9 fusion.19
  337.8 5.4 %pad.128 = f32[2,256,1024]{2,1,0:T(8,128)} pad(f32[2,128,1024]{2,1,0:T(8,128)} %pad_maximum_fusion.2, f32[]{:T(128)} %constant.6.clone.1), padding=0_0_0x0_1_1x0_0_0 | pad | bytes 3145732 | tf_op jit(solution)/shard_map/pad | solution.py:56
  344.1 5.5 %pad.113 = f32[2,256,1024]{2,1,0:T(8,128)} pad(f32[2,128,1024]{2,1,0:T(8,128)} %add.322, f32[]{:T(128)} %constant.6.clone.1), padding=0_0_0x1_0_1x0_0_0 | pad | bytes 3145732 | tf_op jit(solution)/shard_map/pad | solution.py:56
  349.6 2.4 pad_maximum_fusion.1
  351.9 5.5 %pad.112 = f32[2,256,1024]{2,1,0:T(8,128)} pad(f32[2,128,1024]{2,1,0:T(8,128)} %pad_maximum_fusion.1, f32[]{:T(128)} %constant.6.clone.1), padding=0_0_0x0_1_1x0_0_0 | pad | bytes 3145732 | tf_op jit(solution)/shard_map/pad | solution.py:56
  358.4 18.6 %while.12 = (s32[]{:T(128)}, f32[2,1024]{1,0:T(2,128)S(1)}, f32[2,1024]{1,0:T(2,128)}, f32[2,1024]{1,0:T(2,128)S(1)}, f32[2,1024]{1,0:T(2,128)S(1)}, /*index=5*/s32[]{:T(128)}) while((s32[]{:T(128)}, f32[2,1024]{1,0:T(2,128)S(1)}, f32[2,1024]{1,0:T(2,128)}, f32[2,1024]{1,0:T(2,128)S(1)}, f32[2,1024]{1,0:T(2,128)S(1)}, ...), condition=%wide.region_1.0_spmd, body=%wide.region_0.0_spmd.sunk | while | flops 4098 | bytes 98441 | solution.py:65
  358.4 4.4 collective-permute-start
  364.7 4.2 collective-permute-start
  370.8 4.2 collective-permute-start
  377.0 5.8 %fusion.16 = bf16[2,256,1024]{2,1,0:T(8,128)(2,1)} fusion(f32[2,256,1024]{2,1,0:T(8,128)} %bitcast.48, f32[2,256,1024]{2,1,0:T(8,128)} %pad.128, f32[2,256,1024]{2,1,0:T(8,128)S(1)} %copy-done.4, f32[2,256,1024]{2,1,0:T(8,128)} %pad.112, f32[2,256,1024]{2,1,0:T(8,128)} %pad.113, f32[2,1024]{1,0:T(2,128)} %get-tuple-element.28), kind=kLoop, calls=%fused_computation.21 | loop fusion | flops 7340032 | bytes 11542528 | tf_op jit(solution)/shard_map/convert_element_type | solution.py:69
  382.8 6.9 %fusion.35 = f32[512,2048]{1,0:T(8,128)} fusion(bf16[512,1024]{1,0:T(8,128)(2,1)} %bitcast.51, bf16[2048,1024]{1,0:T(8,128)(2,1)} %all-gather.8.cloned.1.call-done), kind=kOutput, calls=%fused_computation.100 | convolution fusion | flops 2147483648 | bytes 9437184 | tf_op jit(solution)/shard_map/dot_general | solution.py:70
  389.7 55.3 %reduce-scatter.2.cloned.1.call-done = f32[512,1024]{1,0:T(8,128)} async-done(((f32[512,2048]{1,0:T(8,128)}), f32[512,1024]{1,0:T(8,128)}) %reduce-scatter.2.cloned.1.call-update) | async-done | bytes 2097168 | tf_op jit(solution)/shard_map/reduce_scatter | solution.py:76
  445.0 2.0 multiply_reduce_fusion
  447.1 1.5 fusion.36
  449.1 4.9 all-reduce.32
  454.1 28.3 %all-reduce.35.cloned.1.call-done = f32[512,362]{0,1:T(8,128)} async-done(((f32[512,362]{0,1:T(8,128)}), f32[512,362]{0,1:T(8,128)}) %all-reduce.35.cloned.1.call-update) | async-done | bytes 741392 | tf_op jit(solution)/shard_map/psum | solution.py:82
  (201 shorter events, 46.5 us)
Async XLA Ops:
  7.2 439.9 %copy-start = (bf16[1024,362]{0,1:T(8,128)(2,1)S(1)}, bf16[1024,362]{0,1:T(8,128)(2,1)}, u32[]{:S(2)}) copy-start(bf16[1024,362]{0,1:T(8,128)(2,1)} %param.22) | copy-start | bytes 2224132
  7.2 2.3 copy-start.33
  7.2 2.3 copy-start.34
  7.2 38.2 %all-gather.6.cloned.1.call-start = ((), (), s32[]{:S(2)}) async-start(), calls=%async_computation.2 | async-start | bytes 3145728 | tf_op jit(solution)/shard_map/all_gather | solution.py:36
  7.9 166.1 %all-gather.4.cloned.1.call-start = ((), (), s32[]{:S(2)}) async-start(), calls=%async_computation.1 | async-start | bytes 17825792 | tf_op jit(solution)/shard_map/all_gather | solution.py:40
  8.7 374.1 %all-gather.8.cloned.1.call-start = ((), (), s32[]{:S(2)}) async-start(), calls=%async_computation.3 | async-start | bytes 4456448 | tf_op jit(solution)/shard_map/all_gather | solution.py:72
  9.4 435.6 %reduce-scatter.2.cloned.1.call-start = ((), (), s32[]{:S(2)}) async-start(), calls=%async_computation.4 | async-start | bytes 6291456 | tf_op jit(solution)/shard_map/reduce_scatter | solution.py:76
  186.6 6.1 %copy-start.35 = (f32[1024]{0:T(1024)S(1)}, f32[1024]{0:T(1024)}, u32[]{:S(2)}) copy-start(f32[1024]{0:T(1024)} %param.20) | copy-start | bytes 12292
  189.5 1.3 copy-start.3
  190.9 3.3 collective-permute-start.1
  299.6 10.6 %copy-start.18 = (f32[2,2,1024]{2,1,0:T(2,128)S(1)}, f32[2,2,1024]{2,1,0:T(2,128)}, u32[]{:S(2)}) copy-start(f32[2,2,1024]{2,1,0:T(2,128)} %slice.335) | copy-start | bytes 49156
  299.6 10.6 %copy-start.19 = (f32[2,2,1024]{2,1,0:T(2,128)S(1)}, f32[2,2,1024]{2,1,0:T(2,128)}, u32[]{:S(2)}) copy-start(f32[2,2,1024]{2,1,0:T(2,128)} %slice.333) | copy-start | bytes 49156
  299.6 10.6 %copy-start.20 = (f32[2,2,1024]{2,1,0:T(2,128)S(1)}, f32[2,2,1024]{2,1,0:T(2,128)}, u32[]{:S(2)}) copy-start(f32[2,2,1024]{2,1,0:T(2,128)} %slice.337) | copy-start | bytes 49156
  299.6 10.8 %copy-start.15 = (f32[1,8,1024]{2,1,0:T(8,128)S(1)}, f32[1,8,1024]{2,1,0:T(8,128)}, u32[]{:S(2)}) copy-start(f32[1,8,1024]{2,1,0:T(8,128)} %get-tuple-element.103) | copy-start | bytes 98308
  299.6 11.1 %copy-start.16 = (f32[2,3,1024]{2,1,0:T(4,128)S(1)}, f32[2,3,1024]{2,1,0:T(4,128)}, u32[]{:S(2)}) copy-start(f32[2,3,1024]{2,1,0:T(4,128)} %slice.326) | copy-start | bytes 73732
  299.6 11.1 %copy-start.17 = (f32[2,3,1024]{2,1,0:T(4,128)S(1)}, f32[2,3,1024]{2,1,0:T(4,128)}, u32[]{:S(2)}) copy-start(f32[2,3,1024]{2,1,0:T(4,128)} %slice.343) | copy-start | bytes 73732
  305.2 5.6 %copy-start.32 = (f32[2,1,1024]{2,1,0:T(1,128)S(1)}, f32[2,1,1024]{2,1,0:T(1,128)}, u32[]{:S(2)}) copy-start(f32[2,1,1024]{2,1,0:T(1,128)} %slice.411) | copy-start | bytes 24580
  305.2 5.7 %copy-start.31 = (f32[2,1,1024]{2,1,0:T(1,128)S(1)}, f32[2,1,1024]{2,1,0:T(1,128)}, u32[]{:S(2)}) copy-start(f32[2,1,1024]{2,1,0:T(1,128)} %slice.385) | copy-start | bytes 24580
  305.2 5.8 %copy-start.13 = (f32[2,7,1024]{2,1,0:T(8,128)S(1)}, f32[2,7,1024]{2,1,0:T(8,128)}, u32[]{:S(2)}) copy-start(f32[2,7,1024]{2,1,0:T(8,128)} %slice.320) | copy-start | bytes 172036
  305.2 5.8 %copy-start.14 = (f32[2,7,1024]{2,1,0:T(8,128)S(1)}, f32[2,7,1024]{2,1,0:T(8,128)}, u32[]{:S(2)}) copy-start(f32[2,7,1024]{2,1,0:T(8,128)} %slice.345) | copy-start | bytes 172036
  305.2 5.9 %copy-start.30 = (f32[2,1,1024]{2,1,0:T(1,128)S(1)}, f32[2,1,1024]{2,1,0:T(1,128)}, u32[]{:S(2)}) copy-start(f32[2,1,1024]{2,1,0:T(1,128)} %slice.410) | copy-start | bytes 24580
  308.2 3.1 copy-start.29
  310.3 1.1 copy-start.11
  310.8 0.7 copy-start.28
  311.1 0.7 copy-start.27
  311.5 1.0 copy-start.9
  311.5 1.0 copy-start.10
  311.9 0.7 copy-start.26
  312.5 0.7 copy-start.25
  313.4 1.2 copy-start.7
  313.4 1.4 copy-start.8
  314.7 1.1 copy-start.24
  318.5 5.5 %copy-start.23 = (f32[2,1,1024]{2,1,0:T(1,128)S(1)}, f32[2,1,1024]{2,1,0:T(1,128)}, u32[]{:S(2)}) copy-start(f32[2,1,1024]{2,1,0:T(1,128)} %slice.381) | copy-start | bytes 24580
  330.9 2.9 copy-start.1
  330.9 2.9 copy-start.2
  330.9 2.9 copy-start.6
  333.7 2.9 copy-start.22
  337.8 5.4 %copy-start.4 = (f32[2,256,1024]{2,1,0:T(8,128)S(1)}, f32[2,256,1024]{2,1,0:T(8,128)}, u32[]{:S(2)}) copy-start(f32[2,256,1024]{2,1,0:T(8,128)} %pad.129) | copy-start | bytes 6291460
  343.2 6.4 %copy-start.21 = (f32[2,1,1024]{2,1,0:T(1,128)S(1)}, f32[2,1,1024]{2,1,0:T(1,128)}, u32[]{:S(2)}) copy-start(f32[2,1,1024]{2,1,0:T(1,128)} %slice.380) | copy-start | bytes 24580
  358.4 5.7 %collective-permute-start = (f32[2,1024]{1,0:T(2,128)S(1)}, f32[2,1024]{1,0:T(2,128)S(1)}, u32[]{:S(2)}, u32[]{:S(2)}) collective-permute-start(f32[2,1024]{1,0:T(2,128)S(1)} %get-tuple-element.135), channel_id=1, source_target_pairs={{0,8},{8,16},{16,24},{1,9},{9,17},{17,25},{2,10},{10,18},{18,26},{... | collective-permute-start | bytes 24584 | tf_op jit(solution)/shard_map/while/body/eval_jaxpr/ppermute | solution.py:13
  364.1 0.6 copy-start.12
  364.7 5.5 %collective-permute-start = (f32[2,1024]{1,0:T(2,128)S(1)}, f32[2,1024]{1,0:T(2,128)S(1)}, u32[]{:S(2)}, u32[]{:S(2)}) collective-permute-start(f32[2,1024]{1,0:T(2,128)S(1)} %get-tuple-element.135), channel_id=1, source_target_pairs={{0,8},{8,16},{16,24},{1,9},{9,17},{17,25},{2,10},{10,18},{18,26},{... | collective-permute-start | bytes 24584 | tf_op jit(solution)/shard_map/while/body/eval_jaxpr/ppermute | solution.py:13
  370.2 0.6 copy-start.12
  370.8 5.5 %collective-permute-start = (f32[2,1024]{1,0:T(2,128)S(1)}, f32[2,1024]{1,0:T(2,128)S(1)}, u32[]{:S(2)}, u32[]{:S(2)}) collective-permute-start(f32[2,1024]{1,0:T(2,128)S(1)} %get-tuple-element.135), channel_id=1, source_target_pairs={{0,8},{8,16},{16,24},{1,9},{9,17},{17,25},{2,10},{10,18},{18,26},{... | collective-permute-start | bytes 24584 | tf_op jit(solution)/shard_map/while/body/eval_jaxpr/ppermute | solution.py:13
  376.4 0.6 copy-start.12
  389.6 55.4 %copy-start.5 = (bf16[2,256,1024]{2,1,0:T(8,128)(2,1)S(1)}, bf16[2,256,1024]{2,1,0:T(8,128)(2,1)}, u32[]{:S(2)}) copy-start(bf16[2,256,1024]{2,1,0:T(8,128)(2,1)} %param.16) | copy-start | bytes 3145732
  389.7 92.7 %all-reduce.35.cloned.1.call-start = ((), (), s32[]{:S(2)}) async-start(), calls=%async_computation.5 | async-start | bytes 1507328 | tf_op jit(solution)/shard_map/psum | solution.py:82
  447.0 1.5 copy-start.38
  447.0 1.6 copy-start.36
  447.0 1.6 copy-start.37
  447.0 1.6 copy-start.39
Sparse Core Ops, SparseCore 0:
  9.6 35.8 all-gather.5
  47.6 126.4 all-gather.3
  176.2 48.9 all-gather.7
  389.8 55.1 reduce-scatter.1
  448.7 33.6 all-reduce.34
where the time goes:
time: 496 us; the launch traced here: 493 us
  waiting for transfers between devices  256 us (52%)
  local copies, waits for them, and re-layouts  133 us (27%)
  other arithmetic  48.4 us (10%)
  matrix products  21.2 us (4%)
  starting transfers between devices  14.7 us (3%)
  between operations  14.6 us (3%)
    all_gather x1, waiting for transfers between devices, shards(): lax.all_gather(w_branches, ('tm', 'batch'), axis=1, tiled=True)  129 us
    slice x52, local copies, waits for them, and re-layouts, shards(): summed, local = lax.associative_scan(link, (log_a, drive), axis=1)  94.9 us
    reduce_scatter x1, waiting for transfers between devices, shards(): lax.psum_scatter(partial_down, 'width', scatter_dimension=1, tiled=True)  55.3 us
    all_gather x1, waiting for transfers between devices, shards(): lax.all_gather(embedded, 'width', axis=2, tiled=True).reshape(count, -1)  35.9 us
    pad x28, local copies, waits for them, and re-layouts, shards(): summed, local = lax.associative_scan(link, (log_a, drive), axis=1)  29.4 us
    psum x1, waiting for transfers between devices, shards(): lax.psum((local_logits, local_value, local_sq), 'width')  28.3 us
    add x13, other arithmetic, link(): return (early[0] + late[0], jnp.exp(late[0]) * early[1] + late[1])  17.8 us
    ppermute x4, starting transfers between devices, from_behind(): lax.ppermute(value, axis, [(source, source + steps) for source in range(i...  14.6 us
  transfers between devices with their start and end apart: 9, of which 8 were waited for; matrix products, arithmetic and copies ran while one was open for 37% of the time, Pallas kernels for 0%

commit v1 on v0

--- a/solution.py
+++ b/solution.py
@@ -30,15 +30,16 @@
     w_policy,
     w_value,
 ):
+
+    def results_spread(incoming_x):
+        return jnp.concatenate(lax.all_gather(incoming_x, ("tm", "batch")), 1)
+
     games, block_len, half = embedded.shape
     count = games * block_len
     chans = w_branches.shape[2]
     features = lax.all_gather(embedded, "width", axis=2, tiled=True).reshape(count, -1)
     proj = jnp.einsum(
-        "td,kdn->ktn",
-        features,
-        lax.all_gather(w_branches, ("tm", "batch"), axis=1, tiled=True),
-        preferred_element_type=jnp.float32,
+        "td,kdn->ktn", features, results_spread(w_branches), preferred_element_type=jnp.float32
     )
     proj = proj.reshape(4, games, block_len, chans)
     gated = jax.nn.gelu(proj[0])

time: 496 us -> 496 us (level)
  waiting for transfers between devices: 256 us -> 240 us
  local copies, waits for them, and re-layouts: 133 us -> 147 us
    all_gather x1, waiting for transfers between devices: 35.9 us -> 18.8 us  [shards(): lax.all_gather(embedded, 'width', axis=2, tiled=True).reshape(count, -1)]
    all_gather x0 -> x1, local copies, waits for them, and re-layouts: none -> 14 us  [results_spread(): return jnp.concatenate(lax.all_gather(incoming_x, ('tm', 'batch')), 1)]
  transfers between devices with their start and end apart: 9 -> 9, of which waited for: 8 -> 8; matrix products, arithmetic and copies ran while one was open for 37% -> 40% of each run, Pallas kernels for 0% -> 0%
where the time goes in v1:
time: 496 us; the launch traced here: 493 us
  waiting for transfers between devices  240 us (48%)
  local copies, waits for them, and re-layouts  147 us (30%)
  other arithmetic  48.4 us (10%)
  matrix products  21.2 us (4%)
  starting transfers between devices  16.6 us (3%)
  between operations  14.6 us (3%)
    all_gather x1, waiting for transfers between devices, results_spread(): return jnp.concatenate(lax.all_gather(incoming_x, ('tm', 'batch')), 1)  130 us
    slice x52, local copies, waits for them, and re-layouts, shards(): summed, local = lax.associative_scan(link, (log_a, drive), axis=1)  94.9 us
    reduce_scatter x1, waiting for transfers between devices, shards(): lax.psum_scatter(partial_down, 'width', scatter_dimension=1, tiled=True)  55.3 us
    pad x28, local copies, waits for them, and re-layouts, shards(): summed, local = lax.associative_scan(link, (log_a, drive), axis=1)  29.4 us
    psum x1, waiting for transfers between devices, shards(): lax.psum((local_logits, local_value, local_sq), 'width')  28.3 us
    all_gather x1, waiting for transfers between devices, shards(): lax.all_gather(embedded, 'width', axis=2, tiled=True).reshape(count, -1)  18.8 us
    add x13, other arithmetic, link(): return (early[0] + late[0], jnp.exp(late[0]) * early[1] + late[1])  17.8 us
    ppermute x4, starting transfers between devices, from_behind(): lax.ppermute(value, axis, [(source, source + steps) for source in range(i...  16.4 us
  transfers between devices with their start and end apart: 9, of which 8 were waited for; matrix products, arithmetic and copies ran while one was open for 40% of the time, Pallas kernels for 0%

profile of v1, /device:TPU:0, one launch (start us, length us, event | category | flops | bytes accessed | tf_op | source)
XLA Modules:
  0.0 492.7 jit_solution(13747978678875757608)
XLA Ops:
  9.5 129.8 %all-gather.9.cloned.1.call-done = bf16[64,128,1024]{2,1,0:T(8,128)(2,1)} async-done(((bf16[4,128,1024]{2,1,0:T(8,128)(2,1)}), bf16[64,128,1024]{2,1,0:T(8,128)(2,1)}) %all-gather.9.cloned.1.call-update) | async-done | bytes 16777232 | tf_op jit(solution)/shard_map/all_gather | solution.py:35
  139.4 14.0 %copy.25 = bf16[16,4,128,1024]{3,2,0,1:T(8,128)(2,1)} copy(bf16[16,4,128,1024]{3,2,1,0:T(8,128)(2,1)} %bitcast.50) | data formatting | bytes 33554432 | tf_op jit(solution)/shard_map/all_gather | solution.py:35
  153.4 18.8 %all-gather.5.cloned.1.call-done = bf16[2,256,2048]{2,1,0:T(8,128)(2,1)} async-done(((bf16[2,256,1024]{2,1,0:T(8,128)(2,1)}), bf16[2,256,2048]{2,1,0:T(8,128)(2,1)}) %all-gather.5.cloned.1.call-update) | async-done | bytes 2097168 | tf_op jit(solution)/shard_map/all_gather | solution.py:40
  172.2 12.5 %convolution_bitcast_fusion = f32[4,512,1024]{2,1,0:T(8,128)S(1)} fusion(bf16[512,2048,1]{1,0,2:T(8,128)(2,1)} %bitcast.81, bf16[4,2048,1024]{2,1,0:T(8,128)(2,1)} %bitcast.51), kind=kOutput, calls=%fused_computation.1 | convolution fusion | flops 8589934592 | bytes 27262976 | tf_op jit(solution)/shard_map/td,kdn->ktn/dot_general | solution.py:41
  184.7 2.9 fusion.30
  189.0 3.6 collective-permute-start.1
  192.6 1.6 collective-permute-done.1
  194.1 7.6 %fusion.4 = (f32[2,256,1024]{2,1,0:T(8,128)S(1)}, f32[2,256,1024]{2,1,0:T(8,128)}) fusion(f32[2,3,1024]{2,1,0:T(4,128)S(1)} %collective-permute-done.1, f32[2,256,1024]{2,1,0:T(8,128)} %bitcast.53, f32[2,256,1024]{2,1,0:T(8,128)} %bitcast.56, f32[1024]{0:T(1024)S(1)} %bitcast.75, f32[1024]{0:T(1024)S(1)} %bitcast.76, f32[1024]{0:T(1024)S(1)} %bitcast.74, ...), kind=kLoop, calls=%fused_computation.9 | loop fusion | flops 12058624 | bytes 10539008 | tf_op jit(solution)/shard_map/mul | solution.py:56
  201.7 2.9 slice.298
  204.6 2.9 slice.299
  207.5 5.4 %slice.297 = f32[2,128,1024]{2,1,0:T(8,128)} slice(f32[2,256,1024]{2,1,0:T(8,128)} %get-tuple-element.48), slice={[0:2:1], [1:256:2], [0:1024:1]} | slice | bytes 2097152 | tf_op jit(solution)/shard_map/slice | solution.py:57
  212.9 5.4 %slice.301 = f32[2,128,1024]{2,1,0:T(8,128)} slice(f32[2,256,1024]{2,1,0:T(8,128)} %get-tuple-element.48), slice={[0:2:1], [0:255:2], [0:1024:1]} | slice | bytes 2097152 | tf_op jit(solution)/shard_map/slice | solution.py:57
  218.3 4.2 multiply_add_fusion.1
  222.5 3.3 slice.304
  225.8 3.3 slice.305
  229.0 3.3 slice.303
  232.3 3.2 slice.307
  235.6 2.5 multiply_add_fusion.2
  239.6 1.7 slice.309
  241.3 1.7 slice.313
  243.0 2.1 multiply_add_fusion.3
  245.1 1.6 slice.316
  246.7 1.6 slice.317
  248.3 1.6 slice.315
  250.0 1.6 slice.319
  251.6 1.8 multiply_add_fusion.4
  254.6 1.5 slice.321
  256.2 1.5 slice.325
  257.7 1.6 multiply_add_fusion.5
  259.3 1.5 slice.329
  260.8 1.5 slice.328
  262.2 1.5 slice.327
  263.7 1.5 slice.331
  270.0 1.5 slice.326
  271.5 1.5 slice.343
  275.8 1.5 slice.320
  278.0 1.4 slice.410
  281.0 1.6 slice.347
  285.5 1.7 slice.308
  290.1 3.3 slice.302
  293.4 3.3 slice.351
  299.6 5.6 %slice.296 = f32[2,127,1024]{2,1,0:T(8,128)} slice(f32[2,256,1024]{2,1,0:T(8,128)} %get-tuple-element.48), slice={[0:2:1], [2:256:2], [0:1024:1]} | slice | bytes 2080768 | tf_op jit(solution)/shard_map/slice | solution.py:57
  305.2 3.0 slice.353
  318.4 5.5 %pad.129 = f32[2,256,1024]{2,1,0:T(8,128)} pad(f32[2,128,1024]{2,1,0:T(8,128)} %add.338, f32[]{:T(128)} %constant.6.clone.1), padding=0_0_0x1_0_1x0_0_0 | pad | bytes 3145732 | tf_op jit(solution)/shard_map/pad | solution.py:57
  323.9 1.9 pad_maximum_fusion.3
  325.8 3.0 pad.110
  328.8 2.0 pad.111
  330.8 2.9 add.322
  333.7 2.9 fusion.19
  337.8 5.4 %pad.128 = f32[2,256,1024]{2,1,0:T(8,128)} pad(f32[2,128,1024]{2,1,0:T(8,128)} %pad_maximum_fusion.2, f32[]{:T(128)} %constant.6.clone.1), padding=0_0_0x0_1_1x0_0_0 | pad | bytes 3145732 | tf_op jit(solution)/shard_map/pad | solution.py:57
  344.1 5.5 %pad.113 = f32[2,256,1024]{2,1,0:T(8,128)} pad(f32[2,128,1024]{2,1,0:T(8,128)} %add.322, f32[]{:T(128)} %constant.6.clone.1), padding=0_0_0x1_0_1x0_0_0 | pad | bytes 3145732 | tf_op jit(solution)/shard_map/pad | solution.py:57
  349.5 2.4 pad_maximum_fusion.1
  351.9 5.5 %pad.112 = f32[2,256,1024]{2,1,0:T(8,128)} pad(f32[2,128,1024]{2,1,0:T(8,128)} %pad_maximum_fusion.1, f32[]{:T(128)} %constant.6.clone.1), padding=0_0_0x0_1_1x0_0_0 | pad | bytes 3145732 | tf_op jit(solution)/shard_map/pad | solution.py:57
  358.3 18.7 %while.12 = (s32[]{:T(128)}, f32[2,1024]{1,0:T(2,128)S(1)}, f32[2,1024]{1,0:T(2,128)}, f32[2,1024]{1,0:T(2,128)S(1)}, f32[2,1024]{1,0:T(2,128)S(1)}, /*index=5*/s32[]{:T(128)}) while((s32[]{:T(128)}, f32[2,1024]{1,0:T(2,128)S(1)}, f32[2,1024]{1,0:T(2,128)}, f32[2,1024]{1,0:T(2,128)S(1)}, f32[2,1024]{1,0:T(2,128)S(1)}, ...), condition=%wide.region_1.0_spmd, body=%wide.region_0.0_spmd.sunk | while | flops 4098 | bytes 98441 | solution.py:66
  358.4 4.5 collective-permute-start
  364.8 4.2 collective-permute-start
  370.9 4.2 collective-permute-start
  377.0 5.8 %fusion.16 = bf16[2,256,1024]{2,1,0:T(8,128)(2,1)} fusion(f32[2,256,1024]{2,1,0:T(8,128)} %bitcast.54, f32[2,256,1024]{2,1,0:T(8,128)} %pad.128, f32[2,256,1024]{2,1,0:T(8,128)S(1)} %copy-done.4, f32[2,256,1024]{2,1,0:T(8,128)} %pad.112, f32[2,256,1024]{2,1,0:T(8,128)} %pad.113, f32[2,1024]{1,0:T(2,128)} %get-tuple-element.28), kind=kLoop, calls=%fused_computation.21 | loop fusion | flops 7340032 | bytes 11542528 | tf_op jit(solution)/shard_map/convert_element_type | solution.py:70
  382.8 6.9 %fusion.35 = f32[512,2048]{1,0:T(8,128)} fusion(bf16[512,1024]{1,0:T(8,128)(2,1)} %bitcast.57, bf16[2048,1024]{1,0:T(8,128)(2,1)} %all-gather.7.cloned.1.call-done), kind=kOutput, calls=%fused_computation.100 | convolution fusion | flops 2147483648 | bytes 9437184 | tf_op jit(solution)/shard_map/dot_general | solution.py:71
  389.8 55.3 %reduce-scatter.2.cloned.1.call-done = f32[512,1024]{1,0:T(8,128)} async-done(((f32[512,2048]{1,0:T(8,128)}), f32[512,1024]{1,0:T(8,128)}) %reduce-scatter.2.cloned.1.call-update) | async-done | bytes 2097168 | tf_op jit(solution)/shard_map/reduce_scatter | solution.py:77
  445.0 2.0 multiply_reduce_fusion
  447.1 1.5 fusion.36
  449.1 4.9 all-reduce.32
  454.1 28.3 %all-reduce.35.cloned.1.call-done = f32[512,362]{0,1:T(8,128)} async-done(((f32[512,362]{0,1:T(8,128)}), f32[512,362]{0,1:T(8,128)}) %all-reduce.35.cloned.1.call-update) | async-done | bytes 741392 | tf_op jit(solution)/shard_map/psum | solution.py:83
  (202 shorter events, 48.0 us)
Async XLA Ops:
  7.2 439.9 %copy-start = (bf16[1024,362]{0,1:T(8,128)(2,1)S(1)}, bf16[1024,362]{0,1:T(8,128)(2,1)}, u32[]{:S(2)}) copy-start(bf16[1024,362]{0,1:T(8,128)(2,1)} %param.22) | copy-start | bytes 2224132
  7.2 2.3 copy-start.33
  7.2 2.3 copy-start.34
  7.2 132.2 %all-gather.9.cloned.1.call-start = ((), (), s32[]{:S(2)}) async-start(), calls=%async_computation.5 | async-start | bytes 17825792 | tf_op jit(solution)/shard_map/all_gather | solution.py:35
  7.9 164.3 %all-gather.5.cloned.1.call-start = ((), (), s32[]{:S(2)}) async-start(), calls=%async_computation.1 | async-start | bytes 3145728 | tf_op jit(solution)/shard_map/all_gather | solution.py:40
  8.7 374.1 %all-gather.7.cloned.1.call-start = ((), (), s32[]{:S(2)}) async-start(), calls=%async_computation.2 | async-start | bytes 4456448 | tf_op jit(solution)/shard_map/all_gather | solution.py:73
  9.4 435.6 %reduce-scatter.2.cloned.1.call-start = ((), (), s32[]{:S(2)}) async-start(), calls=%async_computation.3 | async-start | bytes 6291456 | tf_op jit(solution)/shard_map/reduce_scatter | solution.py:77
  184.7 7.8 %copy-start.35 = (f32[1024]{0:T(1024)S(1)}, f32[1024]{0:T(1024)}, u32[]{:S(2)}) copy-start(f32[1024]{0:T(1024)} %param.20) | copy-start | bytes 12292
  187.6 1.3 copy-start.3
  189.0 5.2 %collective-permute-start.1 = (f32[2,3,1024]{2,1,0:T(4,128)S(1)}, f32[2,3,1024]{2,1,0:T(4,128)S(1)}, u32[]{:S(2)}, u32[]{:S(2)}) collective-permute-start(f32[2,3,1024]{2,1,0:T(4,128)S(1)} %slice.375), channel_id=1, source_target_pairs={{0,8},{8,16},{16,24},{1,9},{9,17},{17,25},{2,10},{10,18},{18,26},{... | collective-permute-start | bytes 73736 | tf_op jit(solution)/shard_map/ppermute | solution.py:13
  299.6 10.6 %copy-start.18 = (f32[2,2,1024]{2,1,0:T(2,128)S(1)}, f32[2,2,1024]{2,1,0:T(2,128)}, u32[]{:S(2)}) copy-start(f32[2,2,1024]{2,1,0:T(2,128)} %slice.335) | copy-start | bytes 49156
  299.6 10.6 %copy-start.19 = (f32[2,2,1024]{2,1,0:T(2,128)S(1)}, f32[2,2,1024]{2,1,0:T(2,128)}, u32[]{:S(2)}) copy-start(f32[2,2,1024]{2,1,0:T(2,128)} %slice.333) | copy-start | bytes 49156
  299.6 10.6 %copy-start.20 = (f32[2,2,1024]{2,1,0:T(2,128)S(1)}, f32[2,2,1024]{2,1,0:T(2,128)}, u32[]{:S(2)}) copy-start(f32[2,2,1024]{2,1,0:T(2,128)} %slice.337) | copy-start | bytes 49156
  299.6 10.8 %copy-start.15 = (f32[1,8,1024]{2,1,0:T(8,128)S(1)}, f32[1,8,1024]{2,1,0:T(8,128)}, u32[]{:S(2)}) copy-start(f32[1,8,1024]{2,1,0:T(8,128)} %get-tuple-element.103) | copy-start | bytes 98308
  299.6 11.1 %copy-start.16 = (f32[2,3,1024]{2,1,0:T(4,128)S(1)}, f32[2,3,1024]{2,1,0:T(4,128)}, u32[]{:S(2)}) copy-start(f32[2,3,1024]{2,1,0:T(4,128)} %slice.326) | copy-start | bytes 73732
  299.6 11.1 %copy-start.17 = (f32[2,3,1024]{2,1,0:T(4,128)S(1)}, f32[2,3,1024]{2,1,0:T(4,128)}, u32[]{:S(2)}) copy-start(f32[2,3,1024]{2,1,0:T(4,128)} %slice.343) | copy-start | bytes 73732
  305.2 5.6 %copy-start.32 = (f32[2,1,1024]{2,1,0:T(1,128)S(1)}, f32[2,1,1024]{2,1,0:T(1,128)}, u32[]{:S(2)}) copy-start(f32[2,1,1024]{2,1,0:T(1,128)} %slice.411) | copy-start | bytes 24580
  305.2 5.7 %copy-start.31 = (f32[2,1,1024]{2,1,0:T(1,128)S(1)}, f32[2,1,1024]{2,1,0:T(1,128)}, u32[]{:S(2)}) copy-start(f32[2,1,1024]{2,1,0:T(1,128)} %slice.385) | copy-start | bytes 24580
  305.2 5.8 %copy-start.13 = (f32[2,7,1024]{2,1,0:T(8,128)S(1)}, f32[2,7,1024]{2,1,0:T(8,128)}, u32[]{:S(2)}) copy-start(f32[2,7,1024]{2,1,0:T(8,128)} %slice.320) | copy-start | bytes 172036
  305.2 5.8 %copy-start.14 = (f32[2,7,1024]{2,1,0:T(8,128)S(1)}, f32[2,7,1024]{2,1,0:T(8,128)}, u32[]{:S(2)}) copy-start(f32[2,7,1024]{2,1,0:T(8,128)} %slice.345) | copy-start | bytes 172036
  305.2 5.9 %copy-start.30 = (f32[2,1,1024]{2,1,0:T(1,128)S(1)}, f32[2,1,1024]{2,1,0:T(1,128)}, u32[]{:S(2)}) copy-start(f32[2,1,1024]{2,1,0:T(1,128)} %slice.410) | copy-start | bytes 24580
  308.2 3.1 copy-start.29
  310.3 1.1 copy-start.11
  310.8 0.7 copy-start.28
  311.0 0.7 copy-start.27
  311.4 1.0 copy-start.9
  311.4 1.0 copy-start.10
  311.9 0.7 copy-start.26
  312.5 0.7 copy-start.25
  313.3 1.2 copy-start.7
  313.3 1.4 copy-start.8
  314.7 1.1 copy-start.24
  318.4 5.5 %copy-start.23 = (f32[2,1,1024]{2,1,0:T(1,128)S(1)}, f32[2,1,1024]{2,1,0:T(1,128)}, u32[]{:S(2)}) copy-start(f32[2,1,1024]{2,1,0:T(1,128)} %slice.381) | copy-start | bytes 24580
  330.8 2.9 copy-start.1
  330.8 2.9 copy-start.2
  330.8 2.9 copy-start.6
  333.7 2.9 copy-start.22
  337.8 5.4 %copy-start.4 = (f32[2,256,1024]{2,1,0:T(8,128)S(1)}, f32[2,256,1024]{2,1,0:T(8,128)}, u32[]{:S(2)}) copy-start(f32[2,256,1024]{2,1,0:T(8,128)} %pad.129) | copy-start | bytes 6291460
  343.2 6.4 %copy-start.21 = (f32[2,1,1024]{2,1,0:T(1,128)S(1)}, f32[2,1,1024]{2,1,0:T(1,128)}, u32[]{:S(2)}) copy-start(f32[2,1,1024]{2,1,0:T(1,128)} %slice.380) | copy-start | bytes 24580
  358.4 5.8 %collective-permute-start = (f32[2,1024]{1,0:T(2,128)S(1)}, f32[2,1024]{1,0:T(2,128)S(1)}, u32[]{:S(2)}, u32[]{:S(2)}) collective-permute-start(f32[2,1024]{1,0:T(2,128)S(1)} %get-tuple-element.135), channel_id=1, source_target_pairs={{0,8},{8,16},{16,24},{1,9},{9,17},{17,25},{2,10},{10,18},{18,26},{... | collective-permute-start | bytes 24584 | tf_op jit(solution)/shard_map/while/body/eval_jaxpr/ppermute | solution.py:13
  364.2 0.6 copy-start.12
  364.8 5.5 %collective-permute-start = (f32[2,1024]{1,0:T(2,128)S(1)}, f32[2,1024]{1,0:T(2,128)S(1)}, u32[]{:S(2)}, u32[]{:S(2)}) collective-permute-start(f32[2,1024]{1,0:T(2,128)S(1)} %get-tuple-element.135), channel_id=1, source_target_pairs={{0,8},{8,16},{16,24},{1,9},{9,17},{17,25},{2,10},{10,18},{18,26},{... | collective-permute-start | bytes 24584 | tf_op jit(solution)/shard_map/while/body/eval_jaxpr/ppermute | solution.py:13
  370.3 0.6 copy-start.12
  370.9 5.5 %collective-permute-start = (f32[2,1024]{1,0:T(2,128)S(1)}, f32[2,1024]{1,0:T(2,128)S(1)}, u32[]{:S(2)}, u32[]{:S(2)}) collective-permute-start(f32[2,1024]{1,0:T(2,128)S(1)} %get-tuple-element.135), channel_id=1, source_target_pairs={{0,8},{8,16},{16,24},{1,9},{9,17},{17,25},{2,10},{10,18},{18,26},{... | collective-permute-start | bytes 24584 | tf_op jit(solution)/shard_map/while/body/eval_jaxpr/ppermute | solution.py:13
  376.4 0.6 copy-start.12
  389.7 55.3 %copy-start.5 = (bf16[2,256,1024]{2,1,0:T(8,128)(2,1)S(1)}, bf16[2,256,1024]{2,1,0:T(8,128)(2,1)}, u32[]{:S(2)}) copy-start(bf16[2,256,1024]{2,1,0:T(8,128)(2,1)} %param.16) | copy-start | bytes 3145732
  389.7 92.6 %all-reduce.35.cloned.1.call-start = ((), (), s32[]{:S(2)}) async-start(), calls=%async_computation.4 | async-start | bytes 1507328 | tf_op jit(solution)/shard_map/psum | solution.py:83
  447.0 1.5 copy-start.38
  447.0 1.6 copy-start.36
  447.0 1.6 copy-start.37
  447.0 1.6 copy-start.39
Sparse Core Ops, SparseCore 0:
  10.2 129.1 all-gather.8
  140.9 31.2 all-gather.4
  174.4 50.3 all-gather.6
  389.8 55.1 reduce-scatter.1
  448.7 33.6 all-reduce.34
